TPU v7x, 128 devices: a whole 4x4x4 slice. The times are simulated.
128 devices in a mesh: row: 16 (over x, y), col: 8 (over z, core).
Axes of the slice: x: 4, y: 4, z: 4, core: 2. Of those that a mesh axis runs over, the one named last changes fastest.
Arguments:
- mask: float32 [8192, 8192], P('row', 'col'), may hold values from -6 to 6
- target: bfloat16 [8192, 8192], P('row', 'col'), may hold values from 0 to 1
- live: int32 [16, 16], P('row', 'col'), may hold values from 0 to 1, as said below
- pupils: float32 [2, 12, 144, 144], replicated, may hold values from -8 to 8
- weights: float32 [12], replicated, may hold values from 0.1 to 1
Outputs:
- updated_mask: float32 [8192, 8192], P('row', 'col')
Inputs may be any that keep to these rules, and one draw needn't show every extreme that they name: In each tile row exactly 5 tiles are live and the others are 0; all 2 tiles of at least one device of the row are live.
All inputs are finite; a program needn't handle non-finite values.
Results may differ from a plain program's by a relative error of at most 0.013.
Values may be sent and summed in bfloat16 or wider, within the bound.
A program may use at most 128 MiB of HBM per device.

v0:
```python
from functools import partial
import math

import jax
import jax.numpy as jnp
import numpy as np
from jax import lax
from jax.experimental import pallas as pl
from jax.experimental.pallas import tpu as pltpu
from jax.sharding import PartitionSpec as P

AMBIT = 128
ROWS = 80
LANES = 128

steepness = 4.0
threshold_level = 1.0
step_rate = 8.0


def folded(count, pixels, offset, period, pad):
    half = count // 2
    frequency = np.arange(half + 1)
    place = np.arange(pixels) + offset
    phases = np.mod(frequency[:, None] * place[None, :], period).astype(np.float32)
    angles = phases * np.float32(2.0 * math.pi / period)
    factor = np.float32(1.0 / math.sqrt(period))
    table = np.zeros((2, pad, pixels), np.float32)
    table[0, : half + 1] = np.cos(angles) * factor
    table[1, : half + 1] = np.sin(angles) * factor
    return table.reshape(2 * pad, pixels)


def tables(count, tile):
    extent = tile + 2 * AMBIT
    inner = folded(count, tile, AMBIT, extent, ROWS)
    wide = folded(count, tile, AMBIT, extent, LANES)
    outer = folded(count, extent, 0, extent, ROWS)
    outer_wide = folded(count, extent, 0, extent, LANES)
    half = count // 2
    left = np.zeros((2 * ROWS, count), np.float32)
    right = np.zeros((2 * LANES, count), np.float32)
    for table, pad in ((left, ROWS), (right, LANES)):
        for f in range(half + 1):
            if f < half:
                table[f, half + f] = 1.0
            if f > 0:
                table[pad + f, half - f] = 1.0
    return [
        jnp.asarray(t, jnp.bfloat16)
        for t in (
            inner, inner.T, wide, wide.T, outer, outer.T, outer_wide, outer_wide.T, left, right.T,
        )
    ]


def dot(a, b):
    return jnp.dot(a, b, preferred_element_type=jnp.float32)


def times(ar, ai, br, bi):
    return ar * br - ai * bi, ar * bi + ai * br


def quarter(ref, part, k):
    return (
        ref[part, k, :ROWS, :LANES],
        ref[part, k, :ROWS, LANES:],
        ref[part, k, ROWS:, :LANES],
        ref[part, k, ROWS:, LANES:],
    )


def fold_pupils(pupils, weights, left, right, quads):
    bf = jnp.bfloat16

    def one(k, carry):
        root = jnp.sqrt(jnp.full((1, pupils.shape[3]), weights[k], jnp.float32))
        for part in range(2):
            value = pupils[part, k] * root
            high = value.astype(bf)
            low = (value - high.astype(jnp.float32)).astype(bf)
            moved = [dot(left[...], dot(v, right[...]).astype(bf)) for v in (high, low)]
            quads[part, k] = moved[0] + moved[1]
        return carry

    lax.fori_loop(0, pupils.shape[1], one, 0)


def take_spectrum(window, outer, outer_wide_t, spec):
    bf = jnp.bfloat16
    partial_rows = dot(outer[...], window).astype(bf)
    blocks = dot(partial_rows, outer_wide_t[...])
    cc, cs = blocks[:ROWS, :LANES], blocks[:ROWS, LANES:]
    sc, ss = blocks[ROWS:, :LANES], blocks[ROWS:, LANES:]
    spec[0] = (cc - ss).astype(bf).astype(jnp.float32)
    spec[1] = -((cs + sc).astype(bf).astype(jnp.float32))
    spec[2] = (cc + ss).astype(bf).astype(jnp.float32)
    spec[3] = (cs - sc).astype(bf).astype(jnp.float32)


def amplitude_of(k, quads, spec):
    ar, br, cr, dr = quarter(quads, 0, k)
    ai, bi, ci, di = quarter(quads, 1, k)
    z1r, z1i, z2r, z2i = spec[0], spec[1], spec[2], spec[3]
    ppr, ppi = times(ar, ai, z1r, z1i)
    pnr, pni = times(br, bi, z2r, z2i)
    npr, npi = times(cr, ci, z2r, -z2i)
    nnr, nni = times(dr, di, z1r, -z1i)
    pr, pi, mr, mi = ppr + nnr, ppi + nni, ppr - nnr, ppi - nni
    qr, qi, nr, ni = pnr + npr, pni + npi, pnr - npr, pni - npi
    return jnp.concatenate(
        [
            jnp.concatenate([pr + qr, ni - mi], axis=1),
            jnp.concatenate([-(mi + ni), qr - pr], axis=1),
            jnp.concatenate([pi + qi, mr - nr], axis=1),
            jnp.concatenate([mr + nr, qi - pi], axis=1),
        ],
        axis=0,
    ).astype(jnp.bfloat16)


def gather_adjoint(k, re, im, quads, acc):
    ar, br, cr, dr = quarter(quads, 0, k)
    ai, bi, ci, di = quarter(quads, 1, k)
    ccr, csr, scr, ssr = re[:ROWS, :LANES], re[:ROWS, LANES:], re[ROWS:, :LANES], re[ROWS:, LANES:]
    cci, csi, sci, ssi = im[:ROWS, :LANES], im[:ROWS, LANES:], im[ROWS:, :LANES], im[ROWS:, LANES:]
    er, ei, fr, fi = ccr - ssr, cci - ssi, ccr + ssr, cci + ssi
    gr, gi, hr, hi = csr + scr, csi + sci, csr - scr, csi - sci
    ur, ui = times(ar, -ai, er + gi, ei - gr)
    vr, vi = times(dr, di, er - gi, -(ei + gr))
    acc[0] += ur + vr
    acc[1] += ui + vi
    ur, ui = times(br, -bi, fr - hi, fi + hr)
    vr, vi = times(cr, ci, fr + hi, hr - fi)
    acc[2] += ur + vr
    acc[3] += ui + vi


def spectral_matrix(acc):
    u1r, u1i, u2r, u2i = acc[0], acc[1], acc[2], acc[3]
    return jnp.concatenate(
        [
            jnp.concatenate([u1r + u2r, u2i - u1i], axis=1),
            jnp.concatenate([-(u1i + u2i), u2r - u1r], axis=1),
        ],
        axis=0,
    ).astype(jnp.bfloat16)


def pieces(tile, width):
    low, high = tile + AMBIT, width + AMBIT
    split = tile + 2 * AMBIT
    rows = {-1: ((AMBIT, AMBIT), low), 0: ((AMBIT, tile), AMBIT), 1: ((tile, AMBIT), 0)}
    outs = []
    for slot in range(2):
        for dr in (-1, 1, 0):
            (first, count), place = rows[dr]
            if dr:
                c0, c1 = ((AMBIT, split), (split, high))[slot]
                outs.append((slot, dr, 0, (first, count, c0, c1 - c0), (place, count, c0, c1 - c0)))
            if slot == 0:
                outs.append((0, dr, 1, (first, count, width, AMBIT), (place, count, 0, AMBIT)))
            else:
                outs.append((1, dr, -1, (first, count, AMBIT, AMBIT), (place, count, high, AMBIT)))
    return outs


def rims(tile, width):
    low, high = tile + AMBIT, width + AMBIT
    cut = tile - AMBIT
    outs = []
    for slot in range(2):
        for dr in (-1, 1, 0):
            first, count = ((AMBIT, tile), (low, AMBIT), (0, AMBIT))[dr]
            side = 1 if dr < 0 else 0
            if dr:
                c0, c1 = ((AMBIT, tile), (tile, high))[slot]
                outs.append((slot, dr, 0, (first, count, c0, c1 - c0), ("rows", side, c0 - AMBIT, c1 - c0)))
            dc, c0, other = ((-1, 0, 1), (1, high, 0))[slot]
            if dr:
                outs.append((slot, dr, dc, (first, count, c0, AMBIT), ("corner", 2 * side + other)))
            else:
                outs.append((slot, 0, dc, (first, count, c0, AMBIT), ("cols", other)))
    return outs


def window(ref, place):
    row, rows, col, cols = place
    return ref.at[pl.ds(row, rows), pl.ds(col, cols)]


def kernel(
    grid, live_ref, weight_ref, mask_hbm, goal_hbm, pupil_hbm, *refs,
):
    tables_hbm, refs = refs[:10], refs[10:]
    out_hbm = refs[0]
    held, refs = refs[1:11], refs[11:]
    (
        mask, goal, pupils, quads, ext, total, fields, intensity, slope, spec, acc, section,
        rim, got_rows, got_cols, got_corner, in_sem, halo_send, halo_recv, rim_send, rim_recv, out_sem,
    ) = refs
    inner, inner_t, wide, wide_t, outer, outer_t, outer_wide, outer_wide_t, left, right = held
    bf = jnp.bfloat16
    tile, width = mask.shape
    extent = tile + 2 * AMBIT
    kernels = pupils.shape[1]
    row, col = lax.axis_index("row"), lax.axis_index("col")
    last_row, last_col = grid[0] - 1, grid[1] - 1

    def there(dr, dc):
        ok = jnp.bool_(True)
        if dr:
            ok = row > 0 if dr < 0 else row < last_row
        if dc:
            side = col > 0 if dc < 0 else col < last_col
            ok = jnp.logical_and(ok, side) if dr else side
        return ok

    def only(dr, dc, act):
        pl.when(there(dr, dc))(act)

    cuts = ((0, AMBIT), (tile - AMBIT, AMBIT), (AMBIT, tile - 2 * AMBIT))
    loads = [
        pltpu.make_async_copy(mask_hbm.at[pl.ds(a, n)], mask.at[pl.ds(a, n)], in_sem.at[i])
        for i, (a, n) in enumerate(cuts)
    ]
    loads.append(pltpu.make_async_copy(pupil_hbm, pupils, in_sem.at[3]))
    order = (8, 9, 4, 7, 2, 1, 3, 0, 6, 5)
    at = {}
    for t in order:
        at[t] = len(loads)
        loads.append(pltpu.make_async_copy(tables_hbm[t], held[t], in_sem.at[len(loads)]))
    goal_load = len(loads)
    loads.append(pltpu.make_async_copy(goal_hbm, goal, in_sem.at[goal_load]))
    for load in loads:
        load.start()

    barrier = pltpu.get_barrier_semaphore()
    around = [(dr, dc) for dr in (-1, 0, 1) for dc in (-1, 0, 1) if dr or dc]
    for dr, dc in around:
        only(dr, dc, lambda: pl.semaphore_signal(
            barrier, inc=1, device_id=(row + dr, col + dc), device_id_type=pl.DeviceIdType.MESH))
    for i, (a, n) in enumerate(cuts):
        loads[i].wait()
        ext[pl.ds(AMBIT + a, n), pl.ds(AMBIT, width)] = mask[pl.ds(a, n)].astype(bf)
    tall = 3 - (row == 0).astype(jnp.int32) - (row == last_row).astype(jnp.int32)
    broad = 3 - (col == 0).astype(jnp.int32) - (col == last_col).astype(jnp.int32)
    pl.semaphore_wait(barrier, tall * broad - 1)

    def copies(table, source, target, send, recv):
        outs = []
        for i, (slot, dr, dc, src, dst) in enumerate(table):
            outs.append((slot, dr, dc, pltpu.make_async_remote_copy(
                src_ref=window(source, src), dst_ref=target(dst), send_sem=send.at[i],
                recv_sem=recv.at[i], device_id=(row + dr, col + dc),
                device_id_type=pl.DeviceIdType.MESH)))
        return outs

    def place(dst):
        if dst[0] == "rows":
            return got_rows.at[dst[1], :, pl.ds(dst[2], dst[3])]
        return got_cols.at[dst[1]] if dst[0] == "cols" else got_corner.at[dst[1]]

    halo = copies(pieces(tile, width), ext, lambda dst: window(ext, dst), halo_send, halo_recv)
    back = copies(rims(tile, width), rim, place, rim_send, rim_recv)
    for slot, dr, dc, copy in halo:
        only(dr, dc, copy.start)
    for slot, dr, dc, src, dst in pieces(tile, width):

        def clear():
            ext[pl.ds(dst[0], dst[1]), pl.ds(dst[2], dst[3])] = jnp.zeros((dst[1], dst[3]), bf)

        pl.when(jnp.logical_not(there(-dr, -dc)))(clear)

    loads[3].wait()
    for t in order[:2]:
        loads[at[t]].wait()
    fold_pupils(pupils, weight_ref, left, right, quads)
    for t in order[2:]:
        loads[at[t]].wait()
    loads[goal_load].wait()

    for now in range(2):
        for slot, dr, dc, copy in halo:
            if slot == now:
                only(-dr, -dc, copy.wait_recv)
        base = now * tile
        take_spectrum(ext[:, pl.ds(base, extent)], outer, outer_wide_t, spec)
        intensity[...] = jnp.zeros_like(intensity)
        acc[...] = jnp.zeros_like(acc)

        def forward(k, carry):
            amplitude = amplitude_of(k, quads, spec)
            section = dot(amplitude, wide[...]).astype(bf)
            section_re, section_im = section[: 2 * ROWS], section[2 * ROWS :]
            step = 128
            for first in range(0, tile, step):
                rows = pl.ds(first, step)
                field_re = dot(inner_t[rows], section_re)
                field_im = dot(inner_t[rows], section_im)
                intensity[rows] += field_re * field_re + field_im * field_im
                fields[k, 0, rows] = field_re.astype(bf)
                fields[k, 1, rows] = field_im.astype(bf)
            return carry

        lax.fori_loop(0, kernels, forward, 0)
        resist = 1.0 / (1.0 + jnp.exp(-steepness * (intensity[...] - threshold_level)))
        live = live_ref[0, now].astype(jnp.float32)
        wanted = goal[:, pl.ds(base, tile)].astype(jnp.float32)
        slope[...] = (
            (2.0 * steepness * live) * (resist - wanted) * resist * (1.0 - resist)
        ).astype(bf)

        def backward(k, carry):
            tops = []
            for part in range(2):
                columns = dot(slope[...] * fields[k, part], wide_t[...]).astype(bf)
                tops.append(dot(inner[...], columns))
            gather_adjoint(k, *tops, quads, acc)
            return carry

        lax.fori_loop(0, kernels, backward, 0)
        returned = dot(spectral_matrix(acc), outer_wide[...]).astype(bf)
        for first in (0, tile + AMBIT) + tuple(range(AMBIT, tile + AMBIT, AMBIT)):
            rows = pl.ds(first, AMBIT)
            piece = dot(outer_t[rows], returned)
            edge = first in (0, tile + AMBIT)
            if now == 0:
                total[rows, pl.ds(0, extent)] = piece
                final = piece[:, :tile]
                if edge:
                    rim[rows, pl.ds(0, tile)] = final.astype(bf)
                else:
                    rim[rows, pl.ds(0, AMBIT)] = final[:, :AMBIT].astype(bf)
            else:
                both = total[rows, pl.ds(tile, extent - tile)] + piece[:, : extent - tile]
                total[rows, pl.ds(tile, extent - tile)] = both
                total[rows, pl.ds(extent, tile)] = piece[:, extent - tile :]
                if edge:
                    rim[rows, pl.ds(tile, extent - tile)] = both.astype(bf)
                    rim[rows, pl.ds(extent, tile)] = piece[:, extent - tile :].astype(bf)
                else:
                    rim[rows, pl.ds(width + AMBIT, AMBIT)] = piece[:, tile + AMBIT :].astype(bf)
        for slot, dr, dc, copy in back:
            if slot == now:
                only(dr, dc, copy.start)

    mask[...] = mask[...] - step_rate * total[pl.ds(AMBIT, tile), pl.ds(AMBIT, width)]
    inside = (AMBIT, tile - 2 * AMBIT, AMBIT, width - 2 * AMBIT)

    def put(place, sem):
        return pltpu.make_async_copy(window(mask, place), window(out_hbm, place), out_sem.at[sem])

    areas = (
        inside,
        (0, AMBIT, 0, width),
        (tile - AMBIT, AMBIT, 0, width),
        (AMBIT, tile - 2 * AMBIT, 0, AMBIT),
        (AMBIT, tile - 2 * AMBIT, width - AMBIT, AMBIT),
    )
    puts = [put(a, i) for i, a in enumerate(areas)]
    puts[0].start()
    for now in range(2):
        for (slot, dr, dc, copy), entry in zip(back, rims(tile, width)):
            if slot != now:
                continue
            dst = entry[4]

            def add():
                copy.wait_recv()
                if dst[0] == "rows":
                    spot = (dst[1] * (tile - AMBIT), AMBIT, dst[2], dst[3])
                elif dst[0] == "cols":
                    spot = (0, tile, dst[1] * (width - AMBIT), AMBIT)
                else:
                    spot = (
                        dst[1] // 2 * (tile - AMBIT), AMBIT, dst[1] % 2 * (width - AMBIT), AMBIT)
                r, n, c, m = spot
                mask[pl.ds(r, n), pl.ds(c, m)] -= step_rate * place(dst)[...].astype(jnp.float32)

            only(-dr, -dc, add)
    for p in puts[1:]:
        p.start()
    for p in puts:
        p.wait()
    for slot, dr, dc, copy in halo + back:
        only(dr, dc, copy.wait_send)


def body(grid, mask, target, live, pupils, weights):
    tile, width = mask.shape
    consts = tables(pupils.shape[2], tile)
    kernels = pupils.shape[1]
    bf, f32 = jnp.bfloat16, jnp.float32
    anywhere = pl.BlockSpec(memory_space=pl.ANY)
    smem = pl.BlockSpec(memory_space=pltpu.SMEM)
    extent = tile + 2 * AMBIT
    return pl.pallas_call(
        partial(kernel, grid),
        out_shape=jax.ShapeDtypeStruct(mask.shape, f32),
        in_specs=[smem, smem] + [anywhere] * 13,
        out_specs=anywhere,
        scratch_shapes=[pltpu.VMEM(t.shape, t.dtype) for t in consts]
        + [
            pltpu.VMEM((tile, width), f32),
            pltpu.VMEM((tile, width), bf),
            pltpu.VMEM(pupils.shape, f32),
            pltpu.VMEM((2, kernels, 2 * ROWS, 2 * LANES), f32),
            pltpu.VMEM((extent, width + 2 * AMBIT), bf),
            pltpu.VMEM((extent, width + 2 * AMBIT), f32),
            pltpu.VMEM((kernels, 2, tile, tile), bf),
            pltpu.VMEM((tile, tile), f32),
            pltpu.VMEM((tile, tile), bf),
            pltpu.VMEM((4, ROWS, LANES), f32),
            pltpu.VMEM((4, ROWS, LANES), f32),
            pltpu.VMEM((2, 4 * ROWS, tile), bf),
            pltpu.VMEM((extent, width + 2 * AMBIT), bf),
            pltpu.VMEM((2, AMBIT, width), bf),
            pltpu.VMEM((2, tile, AMBIT), bf),
            pltpu.VMEM((4, AMBIT, AMBIT), bf),
            pltpu.SemaphoreType.DMA((15,)),
            pltpu.SemaphoreType.DMA((10,)),
            pltpu.SemaphoreType.DMA((10,)),
            pltpu.SemaphoreType.DMA((10,)),
            pltpu.SemaphoreType.DMA((10,)),
            pltpu.SemaphoreType.DMA((5,)),
        ],
        compiler_params=pltpu.CompilerParams(
            collective_id=0, has_side_effects=True, vmem_limit_bytes=60 * 1024 * 1024
        ),
    )(live, weights, mask, target, pupils, *consts)


def solution(mesh):
    return jax.shard_map(
        partial(body, (mesh.shape["row"], mesh.shape["col"])),
        mesh=mesh,
        in_specs=(P("row", "col"), P("row", "col"), P("row", "col"), P(), P()),
        out_specs=P("row", "col"),
        check_vma=False,
    )
```

profile of v0, /device:TPU:39, one launch (start us, length us, event | category | flops | bytes accessed | tf_op | source)
XLA Modules:
  0.0 69.8 jit_solution(11623756600646890306)
XLA Ops:
  0.0 66.6 %shard_map.145 = f32[512,1024]{1,0:T(8,128)} custom-call(s32[1,2]{1,0:T(1,128)} %live_ref.1, f32[12]{0:T(128)} %weight_ref.1, f32[512,1024]{1,0:T(8,128)} %mask_hbm.1, bf16[512,1024]{1,0:T(8,128)(2,1)} %goal_hbm.1, f32[2,12,144,144]{3,2,1,0:T(8,128)} %pupil_hbm.1, bf16[160,512]{1,0:T(8,128)(2,1)} %constant.20.clone.refs_0_, ...), custom_call_target="tpu_custom_call" | custom-call | tf_op jit(solution)/shard_map/pallas_call | solution.py:399
  66.6 3.2 %copy.17 = f32[512,1024]{1,0:T(8,128)} copy(f32[512,1024]{1,0:T(8,128)} %shard_map.145) | data formatting | bytes 4194304
where the time goes:
time: 69.9 us; the launch traced here: 69.8 us
  Pallas kernels  66.6 us (95%)
  local copies, waits for them, and re-layouts  3.16 us (5%)
    pallas_call x1, Pallas kernels, body(): pl.pallas_call(partial(kernel, grid), out_shape=jax.ShapeDtypeStruct(mask...  66.6 us
    unnamed x1, local copies, waits for them, and re-layouts  3.16 us

commit v1 on v0

--- a/solution.py
+++ b/solution.py
@@ -16,6 +16,9 @@
 steepness = 4.0
 threshold_level = 1.0
 step_rate = 8.0
+
+UNROLL = 1
+VMEM_LIMIT = 60 * 1024 * 1024
 
 
 def folded(count, pixels, offset, period, pad):
@@ -31,11 +34,34 @@
     return table.reshape(2 * pad, pixels)
 
 
+def grid_table(count, points, period, pad):
+    half = count // 2
+    angles = np.arange(half + 1)[:, None] * np.arange(points)[None, :] * (2.0 * math.pi / points)
+    table = np.zeros((2, pad, points))
+    table[0, : half + 1] = np.cos(angles) / math.sqrt(period)
+    table[1, : half + 1] = np.sin(angles) / math.sqrt(period)
+    return table.reshape(2 * pad, points)
+
+
+def between(count, points, pixels, offset, period):
+    gap = np.arange(pixels)[:, None] + offset - np.arange(points)[None, :] * (period / points)
+    gap = gap * (2.0 * math.pi / period)
+    return (1.0 + 2.0 * sum(np.cos(m * gap) for m in range(1, count + 1))) / points
+
+
+def halves(table):
+    high = table.astype(jnp.bfloat16).astype(np.float64)
+    return high, table - high
+
+
 def tables(count, tile):
     extent = tile + 2 * AMBIT
-    inner = folded(count, tile, AMBIT, extent, ROWS)
-    wide = folded(count, tile, AMBIT, extent, LANES)
-    outer = folded(count, extent, 0, extent, ROWS)
+    rows = -(-(2 * count + 1) // 16) * 16
+    lanes = -(-(2 * count + 1) // 128) * 128
+    grid_rows = grid_table(count, rows, extent, ROWS)
+    grid_lanes = grid_table(count, lanes, extent, LANES)
+    over_rows = between(count, rows, tile, AMBIT, extent)
+    over_lanes = between(count, lanes, tile, AMBIT, extent)
     outer_wide = folded(count, extent, 0, extent, LANES)
     half = count // 2
     left = np.zeros((2 * ROWS, count), np.float32)
@@ -46,16 +72,24 @@
                 table[f, half + f] = 1.0
             if f > 0:
                 table[pad + f, half - f] = 1.0
+    rows_high, rows_low = halves(over_rows)
+    lanes_high, lanes_low = halves(over_lanes.T)
     return [
         jnp.asarray(t, jnp.bfloat16)
         for t in (
-            inner, inner.T, wide, wide.T, outer, outer.T, outer_wide, outer_wide.T, left, right.T,
+            left, right.T, outer_wide, grid_lanes, grid_rows.T, rows_high, rows_low, lanes_high,
+            lanes_low, rows_high.T, grid_rows,
         )
     ]
 
 
 def dot(a, b):
     return jnp.dot(a, b, preferred_element_type=jnp.float32)
+
+
+def split(value):
+    upper = value.astype(jnp.bfloat16)
+    return upper, (value - upper.astype(jnp.float32)).astype(jnp.bfloat16)
 
 
 def times(ar, ai, br, bi):
@@ -78,18 +112,17 @@
         root = jnp.sqrt(jnp.full((1, pupils.shape[3]), weights[k], jnp.float32))
         for part in range(2):
             value = pupils[part, k] * root
-            high = value.astype(bf)
-            low = (value - high.astype(jnp.float32)).astype(bf)
-            moved = [dot(left[...], dot(v, right[...]).astype(bf)) for v in (high, low)]
+            moved = [dot(left[...], dot(v, right[...]).astype(bf)) for v in split(value)]
             quads[part, k] = moved[0] + moved[1]
         return carry
 
     lax.fori_loop(0, pupils.shape[1], one, 0)
 
 
-def take_spectrum(window, outer, outer_wide_t, spec):
+def take_spectrum(window, outer_wide, outer_wide_t, spec):
     bf = jnp.bfloat16
-    partial_rows = dot(outer[...], window).astype(bf)
+    folds = jnp.concatenate([outer_wide[:ROWS], outer_wide[LANES : LANES + ROWS]], axis=0)
+    partial_rows = dot(folds, window).astype(bf)
     blocks = dot(partial_rows, outer_wide_t[...])
     cc, cs = blocks[:ROWS, :LANES], blocks[:ROWS, LANES:]
     sc, ss = blocks[ROWS:, :LANES], blocks[ROWS:, LANES:]
@@ -139,10 +172,13 @@
 
 def spectral_matrix(acc):
     u1r, u1i, u2r, u2i = acc[0], acc[1], acc[2], acc[3]
+    rest = jnp.zeros((LANES - ROWS, 2 * LANES), jnp.float32)
     return jnp.concatenate(
         [
             jnp.concatenate([u1r + u2r, u2i - u1i], axis=1),
+            rest,
             jnp.concatenate([-(u1i + u2i), u2r - u1r], axis=1),
+            rest,
         ],
         axis=0,
     ).astype(jnp.bfloat16)
@@ -193,14 +229,17 @@
 def kernel(
     grid, live_ref, weight_ref, mask_hbm, goal_hbm, pupil_hbm, *refs,
 ):
-    tables_hbm, refs = refs[:10], refs[10:]
-    out_hbm = refs[0]
-    held, refs = refs[1:11], refs[11:]
+    tables_hbm, refs = refs[:11], refs[11:]
+    out = refs[0]
+    held, refs = refs[1:12], refs[12:]
     (
-        mask, goal, pupils, quads, ext, total, fields, intensity, slope, spec, acc, section,
-        rim, got_rows, got_cols, got_corner, in_sem, halo_send, halo_recv, rim_send, rim_recv, out_sem,
+        mask, goal, pupils, quads, ext, total, fields, intensity, slope, sloped, spec, acc,
+        outer_wide_t, grid_lanes_t, over_lanes, high, low, rim, got_rows, got_cols, got_corner, in_sem, halo_send, halo_recv, rim_send, rim_recv,
     ) = refs
-    inner, inner_t, wide, wide_t, outer, outer_t, outer_wide, outer_wide_t, left, right = held
+    (
+        left, right, outer_wide, grid_lanes, grid_rows_t, rows_high, rows_low, lanes_high,
+        lanes_low, over_rows_t, grid_rows,
+    ) = held
     bf = jnp.bfloat16
     tile, width = mask.shape
     extent = tile + 2 * AMBIT
@@ -226,11 +265,9 @@
         for i, (a, n) in enumerate(cuts)
     ]
     loads.append(pltpu.make_async_copy(pupil_hbm, pupils, in_sem.at[3]))
-    order = (8, 9, 4, 7, 2, 1, 3, 0, 6, 5)
-    at = {}
-    for t in order:
-        at[t] = len(loads)
-        loads.append(pltpu.make_async_copy(tables_hbm[t], held[t], in_sem.at[len(loads)]))
+    first_table = len(loads)
+    for source, target in zip(tables_hbm, held):
+        loads.append(pltpu.make_async_copy(source, target, in_sem.at[len(loads)]))
     goal_load = len(loads)
     loads.append(pltpu.make_async_copy(goal_hbm, goal, in_sem.at[goal_load]))
     for load in loads:
@@ -274,57 +311,65 @@
         pl.when(jnp.logical_not(there(-dr, -dc)))(clear)
 
     loads[3].wait()
-    for t in order[:2]:
-        loads[at[t]].wait()
+    for load in loads[first_table : first_table + 2]:
+        load.wait()
     fold_pupils(pupils, weight_ref, left, right, quads)
-    for t in order[2:]:
-        loads[at[t]].wait()
-    loads[goal_load].wait()
+    for load in loads[first_table + 2 :]:
+        load.wait()
+    points = grid_rows.shape[1]
+    outer_wide_t[...] = outer_wide[...].T
+    grid_lanes_t[...] = grid_lanes[...].T
+    over_lanes[...] = lanes_high[...].T
 
     for now in range(2):
         for slot, dr, dc, copy in halo:
             if slot == now:
                 only(-dr, -dc, copy.wait_recv)
         base = now * tile
-        take_spectrum(ext[:, pl.ds(base, extent)], outer, outer_wide_t, spec)
+        take_spectrum(ext[:, pl.ds(base, extent)], outer_wide, outer_wide_t, spec)
         intensity[...] = jnp.zeros_like(intensity)
         acc[...] = jnp.zeros_like(acc)
 
         def forward(k, carry):
-            amplitude = amplitude_of(k, quads, spec)
-            section = dot(amplitude, wide[...]).astype(bf)
-            section_re, section_im = section[: 2 * ROWS], section[2 * ROWS :]
-            step = 128
-            for first in range(0, tile, step):
-                rows = pl.ds(first, step)
-                field_re = dot(inner_t[rows], section_re)
-                field_im = dot(inner_t[rows], section_im)
-                intensity[rows] += field_re * field_re + field_im * field_im
-                fields[k, 0, rows] = field_re.astype(bf)
-                fields[k, 1, rows] = field_im.astype(bf)
+            section = dot(amplitude_of(k, quads, spec), grid_lanes[...]).astype(bf)
+            field_re = dot(grid_rows_t[...], section[: 2 * ROWS])
+            field_im = dot(grid_rows_t[...], section[2 * ROWS :])
+            intensity[...] += field_re * field_re + field_im * field_im
+            fields[k, :points] = field_re.astype(bf)
+            fields[k, points:] = field_im.astype(bf)
             return carry
 
-        lax.fori_loop(0, kernels, forward, 0)
-        resist = 1.0 / (1.0 + jnp.exp(-steepness * (intensity[...] - threshold_level)))
+        lax.fori_loop(0, kernels, forward, 0, unroll=UNROLL)
+        high[...], low[...] = split(intensity[...])
         live = live_ref[0, now].astype(jnp.float32)
-        wanted = goal[:, pl.ds(base, tile)].astype(jnp.float32)
-        slope[...] = (
-            (2.0 * steepness * live) * (resist - wanted) * resist * (1.0 - resist)
-        ).astype(bf)
+        for first in range(0, tile, 128):
+            rows = pl.ds(first, 128)
+            level = dot(rows_high[rows], high[...]) + dot(rows_high[rows], low[...])
+            level = level + dot(rows_low[rows], high[...])
+            upper, lower = split(level)
+            level = dot(upper, lanes_high[...]) + dot(lower, lanes_high[...])
+            level = level + dot(upper, lanes_low[...])
+            resist = 1.0 / (1.0 + jnp.exp(-steepness * (level - threshold_level)))
+            wanted = goal[rows, pl.ds(base, tile)].astype(jnp.float32)
+            slope[rows] = (
+                (2.0 * steepness * live) * (resist - wanted) * resist * (1.0 - resist)
+            ).astype(bf)
+        sloped[...] = dot(dot(over_rows_t[...], slope[...]).astype(bf), over_lanes[...]).astype(bf)
 
         def backward(k, carry):
             tops = []
             for part in range(2):
-                columns = dot(slope[...] * fields[k, part], wide_t[...]).astype(bf)
-                tops.append(dot(inner[...], columns))
+                cotangent = sloped[...] * fields[k, pl.ds(part * points, points)]
+                columns = dot(cotangent, grid_lanes_t[...]).astype(bf)
+                tops.append(dot(grid_rows[...], columns))
             gather_adjoint(k, *tops, quads, acc)
             return carry
 
-        lax.fori_loop(0, kernels, backward, 0)
+        lax.fori_loop(0, kernels, backward, 0, unroll=UNROLL)
         returned = dot(spectral_matrix(acc), outer_wide[...]).astype(bf)
         for first in (0, tile + AMBIT) + tuple(range(AMBIT, tile + AMBIT, AMBIT)):
             rows = pl.ds(first, AMBIT)
-            piece = dot(outer_t[rows], returned)
+            piece = dot(outer_wide_t[rows], returned)
             edge = first in (0, tile + AMBIT)
             if now == 0:
                 total[rows, pl.ds(0, extent)] = piece
@@ -346,21 +391,6 @@
             if slot == now:
                 only(dr, dc, copy.start)
 
-    mask[...] = mask[...] - step_rate * total[pl.ds(AMBIT, tile), pl.ds(AMBIT, width)]
-    inside = (AMBIT, tile - 2 * AMBIT, AMBIT, width - 2 * AMBIT)
-
-    def put(place, sem):
-        return pltpu.make_async_copy(window(mask, place), window(out_hbm, place), out_sem.at[sem])
-
-    areas = (
-        inside,
-        (0, AMBIT, 0, width),
-        (tile - AMBIT, AMBIT, 0, width),
-        (AMBIT, tile - 2 * AMBIT, 0, AMBIT),
-        (AMBIT, tile - 2 * AMBIT, width - AMBIT, AMBIT),
-    )
-    puts = [put(a, i) for i, a in enumerate(areas)]
-    puts[0].start()
     for now in range(2):
         for (slot, dr, dc, copy), entry in zip(back, rims(tile, width)):
             if slot != now:
@@ -377,13 +407,10 @@
                     spot = (
                         dst[1] // 2 * (tile - AMBIT), AMBIT, dst[1] % 2 * (width - AMBIT), AMBIT)
                 r, n, c, m = spot
-                mask[pl.ds(r, n), pl.ds(c, m)] -= step_rate * place(dst)[...].astype(jnp.float32)
+                total[pl.ds(AMBIT + r, n), pl.ds(AMBIT + c, m)] += place(dst)[...].astype(jnp.float32)
 
             only(-dr, -dc, add)
-    for p in puts[1:]:
-        p.start()
-    for p in puts:
-        p.wait()
+    out[...] = total[pl.ds(AMBIT, tile), pl.ds(AMBIT, width)].astype(bf)
     for slot, dr, dc, copy in halo + back:
         only(dr, dc, copy.wait_send)
 
@@ -396,11 +423,13 @@
     anywhere = pl.BlockSpec(memory_space=pl.ANY)
     smem = pl.BlockSpec(memory_space=pltpu.SMEM)
     extent = tile + 2 * AMBIT
-    return pl.pallas_call(
+    points, lanes = consts[10].shape[1], consts[3].shape[1]
+    vmem = pl.BlockSpec(memory_space=pltpu.VMEM)
+    gradient = pl.pallas_call(
         partial(kernel, grid),
-        out_shape=jax.ShapeDtypeStruct(mask.shape, f32),
-        in_specs=[smem, smem] + [anywhere] * 13,
-        out_specs=anywhere,
+        out_shape=jax.ShapeDtypeStruct(mask.shape, bf),
+        in_specs=[smem, smem] + [anywhere] * (3 + len(consts)),
+        out_specs=vmem,
         scratch_shapes=[pltpu.VMEM(t.shape, t.dtype) for t in consts]
         + [
             pltpu.VMEM((tile, width), f32),
@@ -409,27 +438,29 @@
             pltpu.VMEM((2, kernels, 2 * ROWS, 2 * LANES), f32),
             pltpu.VMEM((extent, width + 2 * AMBIT), bf),
             pltpu.VMEM((extent, width + 2 * AMBIT), f32),
-            pltpu.VMEM((kernels, 2, tile, tile), bf),
-            pltpu.VMEM((tile, tile), f32),
+            pltpu.VMEM((kernels, 2 * points, lanes), bf),
+            pltpu.VMEM((points, lanes), f32),
             pltpu.VMEM((tile, tile), bf),
+            pltpu.VMEM((points, lanes), bf),
             pltpu.VMEM((4, ROWS, LANES), f32),
             pltpu.VMEM((4, ROWS, LANES), f32),
-            pltpu.VMEM((2, 4 * ROWS, tile), bf),
+            pltpu.VMEM(consts[2].shape[::-1], bf),
+            pltpu.VMEM(consts[3].shape[::-1], bf),
+            pltpu.VMEM(consts[7].shape[::-1], bf),
+            pltpu.VMEM((points, lanes), bf),
+            pltpu.VMEM((points, lanes), bf),
             pltpu.VMEM((extent, width + 2 * AMBIT), bf),
             pltpu.VMEM((2, AMBIT, width), bf),
             pltpu.VMEM((2, tile, AMBIT), bf),
             pltpu.VMEM((4, AMBIT, AMBIT), bf),
-            pltpu.SemaphoreType.DMA((15,)),
-            pltpu.SemaphoreType.DMA((10,)),
-            pltpu.SemaphoreType.DMA((10,)),
-            pltpu.SemaphoreType.DMA((10,)),
-            pltpu.SemaphoreType.DMA((10,)),
-            pltpu.SemaphoreType.DMA((5,)),
-        ],
+            pltpu.SemaphoreType.DMA((5 + len(consts),)),
+        ]
+        + [pltpu.SemaphoreType.DMA((10,))] * 4,
         compiler_params=pltpu.CompilerParams(
-            collective_id=0, has_side_effects=True, vmem_limit_bytes=60 * 1024 * 1024
+            collective_id=0, has_side_effects=True, vmem_limit_bytes=VMEM_LIMIT
         ),
     )(live, weights, mask, target, pupils, *consts)
+    return mask - step_rate * gradient.astype(f32)
 
 
 def solution(mesh):

time: 69.9 us -> 66.8 us (0.956)
  local copies, waits for them, and re-layouts: 3.16 us -> 0.01 us
  other arithmetic: 0 us -> 3.02 us
  Pallas kernels: 66.6 us -> 63.6 us
    unnamed x1 -> x2, local copies, waits for them, and re-layouts: 3.16 us -> 0.01 us
    sub x0 -> x1, other arithmetic: none -> 3.02 us  [body(): return mask - step_rate * gradient.astype(f32)]
    pallas_call x1, Pallas kernels: 66.6 us -> 63.6 us  [body(): pl.pallas_call(partial(kernel, grid), out_shape=jax.ShapeDtypeStruct(mask...]
where the time goes in v1:
time: 66.8 us; the launch traced here: 66.7 us
  Pallas kernels  63.6 us (95%)
  other arithmetic  3.02 us (5%)
    pallas_call x1, Pallas kernels, body(): pl.pallas_call(partial(kernel, grid), out_shape=jax.ShapeDtypeStruct(mask...  63.6 us
    sub x1, other arithmetic, body(): return mask - step_rate * gradient.astype(f32)  3.02 us

profile of v1, /device:TPU:39, one launch (start us, length us, event | category | flops | bytes accessed | tf_op | source)
XLA Modules:
  0.0 66.7 jit_solution(2087238608042699880)
XLA Ops:
  0.0 0.0 copy-start
  0.0 63.6 %shard_map.154 = bf16[512,1024]{1,0:T(8,128)(2,1)} custom-call(s32[1,2]{1,0:T(1,128)} %live_ref.1, f32[12]{0:T(128)} %weight_ref.1, f32[512,1024]{1,0:T(8,128)} %mask_hbm.1, bf16[512,1024]{1,0:T(8,128)(2,1)} %goal_hbm.1, f32[2,12,144,144]{3,2,1,0:T(8,128)} %pupil_hbm.1, bf16[160,144]{1,0:T(8,128)(2,1)} %constant.24.clone.refs_0_, ...), custom_call_target="tpu_custom_call" | custom-call | tf_op jit(solution)/shard_map/pallas_call | solution.py:428
  63.6 0.0 copy-done
  63.7 3.0 %multiply_subtract_fusion = f32[512,1024]{1,0:T(8,128)} fusion(f32[512,1024]{1,0:T(8,128)S(1)} %copy-done, bf16[512,1024]{1,0:T(8,128)(2,1)} %shard_map.154), kind=kLoop, calls=%fused_computation | loop fusion | flops 1572864 | bytes 5242880 | tf_op jit(solution)/shard_map/sub | solution.py:463
Async XLA Ops:
  0.0 63.6 %copy-start = (f32[512,1024]{1,0:T(8,128)S(1)}, f32[512,1024]{1,0:T(8,128)}, u32[]{:S(2)}) copy-start(f32[512,1024]{1,0:T(8,128)} %mask_hbm.1) | copy-start | bytes 6291460

commit v2 on v1

--- a/solution.py
+++ b/solution.py
@@ -17,7 +17,7 @@
 threshold_level = 1.0
 step_rate = 8.0
 
-UNROLL = 1
+UNROLL = 2
 VMEM_LIMIT = 60 * 1024 * 1024
 
 
@@ -78,7 +78,7 @@
         jnp.asarray(t, jnp.bfloat16)
         for t in (
             left, right.T, outer_wide, grid_lanes, grid_rows.T, rows_high, rows_low, lanes_high,
-            lanes_low, rows_high.T, grid_rows,
+            lanes_low, grid_rows,
         )
     ]
 
@@ -229,16 +229,16 @@
 def kernel(
     grid, live_ref, weight_ref, mask_hbm, goal_hbm, pupil_hbm, *refs,
 ):
-    tables_hbm, refs = refs[:11], refs[11:]
+    tables_hbm, refs = refs[:10], refs[10:]
     out = refs[0]
-    held, refs = refs[1:12], refs[12:]
+    held, refs = refs[1:11], refs[11:]
     (
         mask, goal, pupils, quads, ext, total, fields, intensity, slope, sloped, spec, acc,
-        outer_wide_t, grid_lanes_t, over_lanes, high, low, rim, got_rows, got_cols, got_corner, in_sem, halo_send, halo_recv, rim_send, rim_recv,
+        outer_wide_t, grid_lanes_t, over_lanes, over_rows_t, high, low, rim, got_rows, got_cols, got_corner, in_sem, halo_send, halo_recv, rim_send, rim_recv,
     ) = refs
     (
         left, right, outer_wide, grid_lanes, grid_rows_t, rows_high, rows_low, lanes_high,
-        lanes_low, over_rows_t, grid_rows,
+        lanes_low, grid_rows,
     ) = held
     bf = jnp.bfloat16
     tile, width = mask.shape
@@ -320,6 +320,7 @@
     outer_wide_t[...] = outer_wide[...].T
     grid_lanes_t[...] = grid_lanes[...].T
     over_lanes[...] = lanes_high[...].T
+    over_rows_t[...] = rows_high[...].T
 
     for now in range(2):
         for slot, dr, dc, copy in halo:
@@ -332,8 +333,10 @@
 
         def forward(k, carry):
             section = dot(amplitude_of(k, quads, spec), grid_lanes[...]).astype(bf)
-            field_re = dot(grid_rows_t[...], section[: 2 * ROWS])
-            field_im = dot(grid_rows_t[...], section[2 * ROWS :])
+            both = jnp.concatenate([section[: 2 * ROWS], section[2 * ROWS :]], axis=1)
+            field = dot(grid_rows_t[...], both)
+            lanes = grid_lanes.shape[1]
+            field_re, field_im = field[:, :lanes], field[:, lanes:]
             intensity[...] += field_re * field_re + field_im * field_im
             fields[k, :points] = field_re.astype(bf)
             fields[k, points:] = field_im.astype(bf)
@@ -357,11 +360,13 @@
         sloped[...] = dot(dot(over_rows_t[...], slope[...]).astype(bf), over_lanes[...]).astype(bf)
 
         def backward(k, carry):
-            tops = []
-            for part in range(2):
-                cotangent = sloped[...] * fields[k, pl.ds(part * points, points)]
-                columns = dot(cotangent, grid_lanes_t[...]).astype(bf)
-                tops.append(dot(grid_rows[...], columns))
+            weight = sloped[...]
+            cotangent = jnp.concatenate(
+                [weight * fields[k, :points], weight * fields[k, points:]], axis=0)
+            columns = dot(cotangent, grid_lanes_t[...]).astype(bf)
+            columns = jnp.concatenate([columns[:points], columns[points:]], axis=1)
+            top = dot(grid_rows[...], columns)
+            tops = [top[:, : 2 * LANES], top[:, 2 * LANES :]]
             gather_adjoint(k, *tops, quads, acc)
             return carry
 
@@ -423,7 +428,7 @@
     anywhere = pl.BlockSpec(memory_space=pl.ANY)
     smem = pl.BlockSpec(memory_space=pltpu.SMEM)
     extent = tile + 2 * AMBIT
-    points, lanes = consts[10].shape[1], consts[3].shape[1]
+    points, lanes = consts[9].shape[1], consts[3].shape[1]
     vmem = pl.BlockSpec(memory_space=pltpu.VMEM)
     gradient = pl.pallas_call(
         partial(kernel, grid),
@@ -447,6 +452,7 @@
             pltpu.VMEM(consts[2].shape[::-1], bf),
             pltpu.VMEM(consts[3].shape[::-1], bf),
             pltpu.VMEM(consts[7].shape[::-1], bf),
+            pltpu.VMEM(consts[5].shape[::-1], bf),
             pltpu.VMEM((points, lanes), bf),
             pltpu.VMEM((points, lanes), bf),
             pltpu.VMEM((extent, width + 2 * AMBIT), bf),

time: 66.8 us -> 57.5 us (0.86)
  Pallas kernels: 63.6 us -> 54.3 us
    pallas_call x1, Pallas kernels: 63.6 us -> 54.3 us  [body(): pl.pallas_call(partial(kernel, grid), out_shape=jax.ShapeDtypeStruct(mask...]
where the time goes in v2:
time: 57.5 us; the launch traced here: 57.3 us
  Pallas kernels  54.3 us (94%)
  other arithmetic  3.02 us (5%)
    pallas_call x1, Pallas kernels, body(): pl.pallas_call(partial(kernel, grid), out_shape=jax.ShapeDtypeStruct(mask...  54.3 us
    sub x1, other arithmetic, body(): return mask - step_rate * gradient.astype(f32)  3.02 us

profile of v2, /device:TPU:39, one launch (start us, length us, event | category | flops | bytes accessed | tf_op | source)
XLA Modules:
  0.0 57.3 jit_solution(2830639904909825520)
XLA Ops:
  0.0 0.0 copy-start
  0.0 54.3 %shard_map.145 = bf16[512,1024]{1,0:T(8,128)(2,1)} custom-call(s32[1,2]{1,0:T(1,128)} %live_ref.1, f32[12]{0:T(128)} %weight_ref.1, f32[512,1024]{1,0:T(8,128)} %mask_hbm.1, bf16[512,1024]{1,0:T(8,128)(2,1)} %goal_hbm.1, f32[2,12,144,144]{3,2,1,0:T(8,128)} %pupil_hbm.1, bf16[160,144]{1,0:T(8,128)(2,1)} %constant.22.clone.refs_0_, ...), custom_call_target="tpu_custom_call" | custom-call | tf_op jit(solution)/shard_map/pallas_call | solution.py:433
  54.3 0.0 copy-done
  54.3 3.0 %multiply_subtract_fusion = f32[512,1024]{1,0:T(8,128)} fusion(f32[512,1024]{1,0:T(8,128)S(1)} %copy-done, bf16[512,1024]{1,0:T(8,128)(2,1)} %shard_map.145), kind=kLoop, calls=%fused_computation | loop fusion | flops 1572864 | bytes 5242880 | tf_op jit(solution)/shard_map/sub | solution.py:469
Async XLA Ops:
  0.0 54.3 %copy-start = (f32[512,1024]{1,0:T(8,128)S(1)}, f32[512,1024]{1,0:T(8,128)}, u32[]{:S(2)}) copy-start(f32[512,1024]{1,0:T(8,128)} %mask_hbm.1) | copy-start | bytes 6291460

commit v3 on v2

--- a/solution.py
+++ b/solution.py
@@ -17,7 +17,7 @@
 threshold_level = 1.0
 step_rate = 8.0
 
-UNROLL = 2
+UNROLL = 6
 VMEM_LIMIT = 60 * 1024 * 1024
 
 
@@ -63,22 +63,13 @@
     over_rows = between(count, rows, tile, AMBIT, extent)
     over_lanes = between(count, lanes, tile, AMBIT, extent)
     outer_wide = folded(count, extent, 0, extent, LANES)
-    half = count // 2
-    left = np.zeros((2 * ROWS, count), np.float32)
-    right = np.zeros((2 * LANES, count), np.float32)
-    for table, pad in ((left, ROWS), (right, LANES)):
-        for f in range(half + 1):
-            if f < half:
-                table[f, half + f] = 1.0
-            if f > 0:
-                table[pad + f, half - f] = 1.0
     rows_high, rows_low = halves(over_rows)
     lanes_high, lanes_low = halves(over_lanes.T)
     return [
         jnp.asarray(t, jnp.bfloat16)
         for t in (
-            left, right.T, outer_wide, grid_lanes, grid_rows.T, rows_high, rows_low, lanes_high,
-            lanes_low, grid_rows,
+            outer_wide, grid_lanes, grid_rows.T, rows_high, rows_low, lanes_high, lanes_low,
+            grid_rows,
         )
     ]
 
@@ -105,14 +96,26 @@
     )
 
 
-def fold_pupils(pupils, weights, left, right, quads):
+def one_hot(shape, half, pad, along):
+    place = lax.broadcasted_iota(jnp.int32, shape, along)
+    source = lax.broadcasted_iota(jnp.int32, shape, 1 - along)
+    above = place >= pad
+    wanted = jnp.where(above, half + pad - place, half + place)
+    hit = jnp.logical_and(source == wanted, place != pad)
+    return jnp.where(hit, 1.0, 0.0).astype(jnp.bfloat16)
+
+
+def fold_pupils(pupils, weights, quads):
     bf = jnp.bfloat16
+    count = pupils.shape[3]
+    left = one_hot((2 * ROWS, count), count // 2, ROWS, 0)
+    right = one_hot((count, 2 * LANES), count // 2, LANES, 1)
 
     def one(k, carry):
         root = jnp.sqrt(jnp.full((1, pupils.shape[3]), weights[k], jnp.float32))
         for part in range(2):
             value = pupils[part, k] * root
-            moved = [dot(left[...], dot(v, right[...]).astype(bf)) for v in split(value)]
+            moved = [dot(left, dot(v, right).astype(bf)) for v in split(value)]
             quads[part, k] = moved[0] + moved[1]
         return carry
 
@@ -229,16 +232,15 @@
 def kernel(
     grid, live_ref, weight_ref, mask_hbm, goal_hbm, pupil_hbm, *refs,
 ):
-    tables_hbm, refs = refs[:10], refs[10:]
+    tables_hbm, refs = refs[:8], refs[8:]
     out = refs[0]
-    held, refs = refs[1:11], refs[11:]
+    held, refs = refs[1:9], refs[9:]
     (
         mask, goal, pupils, quads, ext, total, fields, intensity, slope, sloped, spec, acc,
         outer_wide_t, grid_lanes_t, over_lanes, over_rows_t, high, low, rim, got_rows, got_cols, got_corner, in_sem, halo_send, halo_recv, rim_send, rim_recv,
     ) = refs
     (
-        left, right, outer_wide, grid_lanes, grid_rows_t, rows_high, rows_low, lanes_high,
-        lanes_low, grid_rows,
+        outer_wide, grid_lanes, grid_rows_t, rows_high, rows_low, lanes_high, lanes_low, grid_rows,
     ) = held
     bf = jnp.bfloat16
     tile, width = mask.shape
@@ -311,10 +313,8 @@
         pl.when(jnp.logical_not(there(-dr, -dc)))(clear)
 
     loads[3].wait()
-    for load in loads[first_table : first_table + 2]:
-        load.wait()
-    fold_pupils(pupils, weight_ref, left, right, quads)
-    for load in loads[first_table + 2 :]:
+    fold_pupils(pupils, weight_ref, quads)
+    for load in loads[first_table:]:
         load.wait()
     points = grid_rows.shape[1]
     outer_wide_t[...] = outer_wide[...].T
@@ -345,8 +345,8 @@
         lax.fori_loop(0, kernels, forward, 0, unroll=UNROLL)
         high[...], low[...] = split(intensity[...])
         live = live_ref[0, now].astype(jnp.float32)
-        for first in range(0, tile, 128):
-            rows = pl.ds(first, 128)
+        def compare(part, carry):
+            rows = pl.ds(pl.multiple_of(part * 128, 128), 128)
             level = dot(rows_high[rows], high[...]) + dot(rows_high[rows], low[...])
             level = level + dot(rows_low[rows], high[...])
             upper, lower = split(level)
@@ -357,6 +357,9 @@
             slope[rows] = (
                 (2.0 * steepness * live) * (resist - wanted) * resist * (1.0 - resist)
             ).astype(bf)
+            return carry
+
+        lax.fori_loop(0, tile // 128, compare, 0)
         sloped[...] = dot(dot(over_rows_t[...], slope[...]).astype(bf), over_lanes[...]).astype(bf)
 
         def backward(k, carry):
@@ -373,6 +376,10 @@
         lax.fori_loop(0, kernels, backward, 0, unroll=UNROLL)
         returned = dot(spectral_matrix(acc), outer_wide[...]).astype(bf)
         for first in (0, tile + AMBIT) + tuple(range(AMBIT, tile + AMBIT, AMBIT)):
+            if first == AMBIT:
+                for slot, dr, dc, copy in back:
+                    if slot == now and dr:
+                        only(dr, dc, copy.start)
             rows = pl.ds(first, AMBIT)
             piece = dot(outer_wide_t[rows], returned)
             edge = first in (0, tile + AMBIT)
@@ -393,7 +400,7 @@
                 else:
                     rim[rows, pl.ds(width + AMBIT, AMBIT)] = piece[:, tile + AMBIT :].astype(bf)
         for slot, dr, dc, copy in back:
-            if slot == now:
+            if slot == now and not dr:
                 only(dr, dc, copy.start)
 
     for now in range(2):
@@ -428,7 +435,7 @@
     anywhere = pl.BlockSpec(memory_space=pl.ANY)
     smem = pl.BlockSpec(memory_space=pltpu.SMEM)
     extent = tile + 2 * AMBIT
-    points, lanes = consts[9].shape[1], consts[3].shape[1]
+    points, lanes = consts[7].shape[1], consts[1].shape[1]
     vmem = pl.BlockSpec(memory_space=pltpu.VMEM)
     gradient = pl.pallas_call(
         partial(kernel, grid),
@@ -449,10 +456,10 @@
             pltpu.VMEM((points, lanes), bf),
             pltpu.VMEM((4, ROWS, LANES), f32),
             pltpu.VMEM((4, ROWS, LANES), f32),
-            pltpu.VMEM(consts[2].shape[::-1], bf),
+            pltpu.VMEM(consts[0].shape[::-1], bf),
+            pltpu.VMEM(consts[1].shape[::-1], bf),
+            pltpu.VMEM(consts[5].shape[::-1], bf),
             pltpu.VMEM(consts[3].shape[::-1], bf),
-            pltpu.VMEM(consts[7].shape[::-1], bf),
-            pltpu.VMEM(consts[5].shape[::-1], bf),
             pltpu.VMEM((points, lanes), bf),
             pltpu.VMEM((points, lanes), bf),
             pltpu.VMEM((extent, width + 2 * AMBIT), bf),

time: 57.5 us -> 55.1 us (0.958)
  Pallas kernels: 54.3 us -> 51.9 us
    pallas_call x1, Pallas kernels: 54.3 us -> 51.9 us  [body(): pl.pallas_call(partial(kernel, grid), out_shape=jax.ShapeDtypeStruct(mask...]
where the time goes in v3:
time: 55.1 us; the launch traced here: 55 us
  Pallas kernels  51.9 us (94%)
  other arithmetic  3.02 us (5%)
    pallas_call x1, Pallas kernels, body(): pl.pallas_call(partial(kernel, grid), out_shape=jax.ShapeDtypeStruct(mask...  51.9 us
    sub x1, other arithmetic, body(): return mask - step_rate * gradient.astype(f32)  3.02 us

profile of v3, /device:TPU:39, one launch (start us, length us, event | category | flops | bytes accessed | tf_op | source)
XLA Modules:
  0.0 55.0 jit_solution(17238126216232843250)
XLA Ops:
  0.0 0.0 copy-start
  0.0 51.9 %shard_map.127 = bf16[512,1024]{1,0:T(8,128)(2,1)} custom-call(s32[1,2]{1,0:T(1,128)} %live_ref.1, f32[12]{0:T(128)} %weight_ref.1, f32[512,1024]{1,0:T(8,128)} %mask_hbm.1, bf16[512,1024]{1,0:T(8,128)(2,1)} %goal_hbm.1, f32[2,12,144,144]{3,2,1,0:T(8,128)} %pupil_hbm.1, bf16[256,768]{1,0:T(8,128)(2,1)} %constant.18.clone.refs_0_, ...), custom_call_target="tpu_custom_call" | custom-call | tf_op jit(solution)/shard_map/pallas_call | solution.py:440
  51.9 0.0 copy-done
  51.9 3.0 %multiply_subtract_fusion = f32[512,1024]{1,0:T(8,128)} fusion(f32[512,1024]{1,0:T(8,128)S(1)} %copy-done, bf16[512,1024]{1,0:T(8,128)(2,1)} %shard_map.127), kind=kLoop, calls=%fused_computation | loop fusion | flops 1572864 | bytes 5242880 | tf_op jit(solution)/shard_map/sub | solution.py:476
Async XLA Ops:
  0.0 51.9 %copy-start = (f32[512,1024]{1,0:T(8,128)S(1)}, f32[512,1024]{1,0:T(8,128)}, u32[]{:S(2)}) copy-start(f32[512,1024]{1,0:T(8,128)} %mask_hbm.1) | copy-start | bytes 6291460

commit v4 on v3

--- a/solution.py
+++ b/solution.py
@@ -272,7 +272,7 @@
         loads.append(pltpu.make_async_copy(source, target, in_sem.at[len(loads)]))
     goal_load = len(loads)
     loads.append(pltpu.make_async_copy(goal_hbm, goal, in_sem.at[goal_load]))
-    for load in loads:
+    for load in loads[:3]:
         load.start()
 
     barrier = pltpu.get_barrier_semaphore()
@@ -280,9 +280,15 @@
     for dr, dc in around:
         only(dr, dc, lambda: pl.semaphore_signal(
             barrier, inc=1, device_id=(row + dr, col + dc), device_id_type=pl.DeviceIdType.MESH))
-    for i, (a, n) in enumerate(cuts):
+    def take(i):
+        start, count = cuts[i]
         loads[i].wait()
-        ext[pl.ds(AMBIT + a, n), pl.ds(AMBIT, width)] = mask[pl.ds(a, n)].astype(bf)
+        ext[pl.ds(AMBIT + start, count), pl.ds(AMBIT, width)] = mask[pl.ds(start, count)].astype(bf)
+
+    take(0)
+    take(1)
+    for load in loads[3:]:
+        load.start()
     tall = 3 - (row == 0).astype(jnp.int32) - (row == last_row).astype(jnp.int32)
     broad = 3 - (col == 0).astype(jnp.int32) - (col == last_col).astype(jnp.int32)
     pl.semaphore_wait(barrier, tall * broad - 1)
@@ -304,7 +310,12 @@
     halo = copies(pieces(tile, width), ext, lambda dst: window(ext, dst), halo_send, halo_recv)
     back = copies(rims(tile, width), rim, place, rim_send, rim_recv)
     for slot, dr, dc, copy in halo:
-        only(dr, dc, copy.start)
+        if dr:
+            only(dr, dc, copy.start)
+    take(2)
+    for slot, dr, dc, copy in halo:
+        if not dr:
+            only(dr, dc, copy.start)
     for slot, dr, dc, src, dst in pieces(tile, width):
 
         def clear():
@@ -403,6 +414,11 @@
             if slot == now and not dr:
                 only(dr, dc, copy.start)
 
+    def leave(r, n, c, m):
+        out[pl.ds(r, n), pl.ds(c, m)] = total[pl.ds(AMBIT + r, n), pl.ds(AMBIT + c, m)].astype(bf)
+
+    inner_rows = tile - 2 * AMBIT
+    leave(AMBIT, inner_rows, AMBIT, width - 2 * AMBIT)
     for now in range(2):
         for (slot, dr, dc, copy), entry in zip(back, rims(tile, width)):
             if slot != now:
@@ -422,7 +438,10 @@
                 total[pl.ds(AMBIT + r, n), pl.ds(AMBIT + c, m)] += place(dst)[...].astype(jnp.float32)
 
             only(-dr, -dc, add)
-    out[...] = total[pl.ds(AMBIT, tile), pl.ds(AMBIT, width)].astype(bf)
+    leave(0, AMBIT, 0, width)
+    leave(tile - AMBIT, AMBIT, 0, width)
+    leave(AMBIT, inner_rows, 0, AMBIT)
+    leave(AMBIT, inner_rows, width - AMBIT, AMBIT)
     for slot, dr, dc, copy in halo + back:
         only(dr, dc, copy.wait_send)
 

time: 55.1 us -> 55.1 us (level)
  no operation moved by 1% of the time
where the time goes in v4:
time: 55.1 us; the launch traced here: 54.9 us
  Pallas kernels  51.9 us (94%)
  other arithmetic  3.02 us (5%)
    pallas_call x1, Pallas kernels, body(): pl.pallas_call(partial(kernel, grid), out_shape=jax.ShapeDtypeStruct(mask...  51.9 us
    sub x1, other arithmetic, body(): return mask - step_rate * gradient.astype(f32)  3.02 us

profile of v4, /device:TPU:39, one launch (start us, length us, event | category | flops | bytes accessed | tf_op | source)
XLA Modules:
  0.0 54.9 jit_solution(12039371888217563180)
XLA Ops:
  0.0 0.0 copy-start
  0.0 51.9 %shard_map.127 = bf16[512,1024]{1,0:T(8,128)(2,1)} custom-call(s32[1,2]{1,0:T(1,128)} %live_ref.1, f32[12]{0:T(128)} %weight_ref.1, f32[512,1024]{1,0:T(8,128)} %mask_hbm.1, bf16[512,1024]{1,0:T(8,128)(2,1)} %goal_hbm.1, f32[2,12,144,144]{3,2,1,0:T(8,128)} %pupil_hbm.1, bf16[256,768]{1,0:T(8,128)(2,1)} %constant.18.clone.refs_0_, ...), custom_call_target="tpu_custom_call" | custom-call | tf_op jit(solution)/shard_map/pallas_call | solution.py:459
  51.9 0.0 copy-done
  51.9 3.0 %multiply_subtract_fusion = f32[512,1024]{1,0:T(8,128)} fusion(f32[512,1024]{1,0:T(8,128)S(1)} %copy-done, bf16[512,1024]{1,0:T(8,128)(2,1)} %shard_map.127), kind=kLoop, calls=%fused_computation | loop fusion | flops 1572864 | bytes 5242880 | tf_op jit(solution)/shard_map/sub | solution.py:495
Async XLA Ops:
  0.0 51.9 %copy-start = (f32[512,1024]{1,0:T(8,128)S(1)}, f32[512,1024]{1,0:T(8,128)}, u32[]{:S(2)}) copy-start(f32[512,1024]{1,0:T(8,128)} %mask_hbm.1) | copy-start | bytes 6291460

commit v5 on v4

--- a/solution.py
+++ b/solution.py
@@ -272,7 +272,7 @@
         loads.append(pltpu.make_async_copy(source, target, in_sem.at[len(loads)]))
     goal_load = len(loads)
     loads.append(pltpu.make_async_copy(goal_hbm, goal, in_sem.at[goal_load]))
-    for load in loads[:3]:
+    for load in loads[:4]:
         load.start()
 
     barrier = pltpu.get_barrier_semaphore()
@@ -287,7 +287,7 @@
 
     take(0)
     take(1)
-    for load in loads[3:]:
+    for load in loads[4:]:
         load.start()
     tall = 3 - (row == 0).astype(jnp.int32) - (row == last_row).astype(jnp.int32)
     broad = 3 - (col == 0).astype(jnp.int32) - (col == last_col).astype(jnp.int32)

time: 55.1 us -> 55.1 us (level)
  no operation moved by 1% of the time
where the time goes in v5:
time: 55.1 us; the launch traced here: 54.9 us
  Pallas kernels  51.9 us (94%)
  other arithmetic  3.02 us (5%)
    pallas_call x1, Pallas kernels, body(): pl.pallas_call(partial(kernel, grid), out_shape=jax.ShapeDtypeStruct(mask...  51.9 us
    sub x1, other arithmetic, body(): return mask - step_rate * gradient.astype(f32)  3.02 us

profile of v5, /device:TPU:39, one launch (start us, length us, event | category | flops | bytes accessed | tf_op | source)
XLA Modules:
  0.0 54.9 jit_solution(6617886437309282561)
XLA Ops:
  0.0 0.0 copy-start
  0.0 51.9 %shard_map.127 = bf16[512,1024]{1,0:T(8,128)(2,1)} custom-call(s32[1,2]{1,0:T(1,128)} %live_ref.1, f32[12]{0:T(128)} %weight_ref.1, f32[512,1024]{1,0:T(8,128)} %mask_hbm.1, bf16[512,1024]{1,0:T(8,128)(2,1)} %goal_hbm.1, f32[2,12,144,144]{3,2,1,0:T(8,128)} %pupil_hbm.1, bf16[256,768]{1,0:T(8,128)(2,1)} %constant.18.clone.refs_0_, ...), custom_call_target="tpu_custom_call" | custom-call | tf_op jit(solution)/shard_map/pallas_call | solution.py:459
  51.9 0.0 copy-done
  51.9 3.0 %multiply_subtract_fusion = f32[512,1024]{1,0:T(8,128)} fusion(f32[512,1024]{1,0:T(8,128)S(1)} %copy-done, bf16[512,1024]{1,0:T(8,128)(2,1)} %shard_map.127), kind=kLoop, calls=%fused_computation | loop fusion | flops 1572864 | bytes 5242880 | tf_op jit(solution)/shard_map/sub | solution.py:495
Async XLA Ops:
  0.0 51.9 %copy-start = (f32[512,1024]{1,0:T(8,128)S(1)}, f32[512,1024]{1,0:T(8,128)}, u32[]{:S(2)}) copy-start(f32[512,1024]{1,0:T(8,128)} %mask_hbm.1) | copy-start | bytes 6291460
